TPU v7x, 32 devices: a whole 2x2x4 slice. The times are simulated.
32 devices in a mesh: fsdp: 16 (over z, x, core), tp: 2 (over y).
Axes of the slice: x: 2, y: 2, z: 4, core: 2. Of those that a mesh axis runs over, the one named last changes fastest.
Arguments:
- saved_master: float32 [16384, 5120], P(('fsdp', 'tp')), may hold values from -6 to 6
- saved_first: float32 [16384, 5120], P(('fsdp', 'tp')), may hold values from -6 to 6
- saved_second: float32 [16384, 5120], P(('fsdp', 'tp')), may hold values from 0.05 to 20
- grad: bfloat16 [16384, 5120], P('fsdp', 'tp'), may hold values from -10000 to 10000
- row_target: int32 [16384], replicated, may hold values from 0 to 16383, as said below
- step: int32 [1], replicated, may hold values from 1 to 63
Outputs:
- new_master: float32 [16384, 5120], P('fsdp', 'tp')
- new_first: float32 [16384, 5120], P('fsdp', 'tp')
- new_second: float32 [16384, 5120], P('fsdp', 'tp')
- direction: float32 [16384, 5120], P('fsdp', 'tp')
Inputs may be any that keep to these rules, and one draw needn't show every extreme that they name: `row_target`: a permutation of 0 to 16383; the saved rows j * 1024 to (j + 1) * 1024 - 1 of every block j send exactly 64 rows into every new block of 1024 rows.
All inputs are finite; a program needn't handle non-finite values.
Results may differ from a plain program's by a relative error of at most 0.0003.
Values sent between devices are 32-bit elements; how exact they have to be, the bound alone decides.
A program may use at most 192 MiB of HBM per device.

v0:
```python
import math

import jax
import jax.numpy as jnp
from jax import lax
from jax.sharding import PartitionSpec as P

H = 16384
D = 5120


beta_one = 0.9
beta_two = 0.95
epsilon = 1e-08
learn_rate = 0.001
weight_decay = 0.1


def adam_update(master, first, second, grad, scale, step):
    clipped = scale * grad.astype(jnp.float32)
    first_new = beta_one * first + (1.0 - beta_one) * clipped
    second_new = beta_two * second + (1.0 - beta_two) * clipped * clipped
    count = step[0].astype(jnp.float32)
    first_hat = first_new / (1.0 - jnp.power(jnp.float32(beta_one), count))
    second_hat = second_new / (1.0 - jnp.power(jnp.float32(beta_two), count))
    direction = first_hat / (jnp.sqrt(second_hat) + epsilon) + weight_decay * master
    return (master - learn_rate * direction, first_new, second_new, direction)


def per_device(saved_master, saved_first, saved_second, grad, row_target, step):
    tp_count = lax.axis_size("tp")
    fsdp_count = lax.axis_size("fsdp")
    block_index = lax.axis_index("fsdp")
    block_rows = grad.shape[0]
    all_rows = row_target.shape[0]
    grad_wide = grad.astype(jnp.float32)
    local_square = jnp.sum(grad_wide * grad_wide)
    mine = lax.dynamic_slice_in_dim(row_target, block_index * block_rows, block_rows)
    send_order = jnp.argsort(mine, stable=True)
    positions = jnp.arange(all_rows, dtype=jnp.int32)
    in_block = row_target // block_rows == block_index
    sort_keys = jnp.where(
        in_block, positions // block_rows * all_rows + row_target, all_rows * all_rows
    )
    picked = jnp.argsort(sort_keys, stable=True)[:block_rows]
    arrived_rows = row_target[picked] - block_index * block_rows
    place_order = jnp.argsort(arrived_rows, stable=True)
    tp_copies = jnp.full((1, tp_count), local_square, jnp.float32)
    middle = (
        lax.all_to_all(saved_master, "tp", split_axis=1, concat_axis=0, tiled=True),
        lax.all_to_all(saved_first, "tp", split_axis=1, concat_axis=0, tiled=True),
        lax.all_to_all(saved_second, "tp", split_axis=1, concat_axis=0, tiled=True),
        lax.all_to_all(tp_copies, "tp", split_axis=1, concat_axis=0, tiled=True),
    )
    row_square = jnp.sum(middle[3])
    fsdp_copies = jnp.full((fsdp_count, 1), row_square, jnp.float32)
    arrived = (
        lax.all_to_all(middle[0][send_order], "fsdp", split_axis=0, concat_axis=0, tiled=True),
        lax.all_to_all(middle[1][send_order], "fsdp", split_axis=0, concat_axis=0, tiled=True),
        lax.all_to_all(middle[2][send_order], "fsdp", split_axis=0, concat_axis=0, tiled=True),
        lax.all_to_all(fsdp_copies, "fsdp", split_axis=0, concat_axis=0, tiled=True),
    )
    total = jnp.sum(arrived[3])
    master = arrived[0][place_order]
    first = arrived[1][place_order]
    second = arrived[2][place_order]
    scale = jnp.minimum(1.0, math.sqrt(H * D) / jnp.sqrt(total))
    return adam_update(master, first, second, grad, scale, step)


def solution(mesh):
    in_specs = (
        P(("fsdp", "tp"), None),
        P(("fsdp", "tp"), None),
        P(("fsdp", "tp"), None),
        P("fsdp", "tp"),
        P(),
        P(),
    )
    out_specs = (P("fsdp", "tp"), P("fsdp", "tp"), P("fsdp", "tp"), P("fsdp", "tp"))
    return jax.shard_map(
        per_device, mesh=mesh, in_specs=in_specs, out_specs=out_specs, check_vma=False
    )
```

profile of v0, /device:TPU:11, one launch (start us, length us, event | category | flops | bytes accessed | tf_op | source)
XLA Modules:
  0.0 1137.6 jit_solution(8352183307849591315)
XLA Ops:
  0.6 5.8 fusion.2
  6.4 0.6 broadcast_in_dim.27
  7.1 5.0 all_to_all.109
  12.0 0.6 reduce_sum.28
  12.6 1.2 broadcast_in_dim.28
  13.9 7.9 all-to-all-start.5
  21.8 8.9 copy.34
  30.7 0.0 all-to-all-done.5
  30.7 7.7 all-to-all-start.2
  38.4 8.9 copy.33
  47.4 105.6 %all-to-all-done.2 = f32[512,2,2560]{2,0,1:T(8,128)} async-done(((f32[512,2,2560]{2,0,1:T(8,128)}), f32[512,2,2560]{2,0,1:T(8,128)}, u32[]{:S(2)}, u32[]{:S(2)}) %all-to-all-start.2) | async-done | bytes 10485792 | tf_op jit(solution)/shard_map/all_to_all | solution.py:51
  152.9 7.7 all-to-all-start.6
  160.7 8.9 copy.35
  169.6 104.7 %all-to-all-done.6 = f32[512,2,2560]{2,0,1:T(8,128)} async-done(((f32[512,2,2560]{2,0,1:T(8,128)}), f32[512,2,2560]{2,0,1:T(8,128)}, u32[]{:S(2)}, u32[]{:S(2)}) %all-to-all-start.6) | async-done | bytes 10485792 | tf_op jit(solution)/shard_map/all_to_all | solution.py:52
  274.3 0.0 copy-start
  274.3 7.8 all-to-all-start
  282.2 0.0 copy-done
  282.2 4.4 sort.48
  286.6 14.2 %gather_fusion.3 = f32[1024,2560]{1,0:T(8,128)} fusion(f32[1024,2560]{1,0:T(8,128)} %bitcast.5, s32[1024]{0:T(1024)S(1)} %fusion.13), kind=kCustom, calls=%fused_computation.3 | custom fusion | bytes 20975616 | tf_op jit(solution)/shard_map/gather | solution.py:59
  300.8 94.1 %all-to-all-done = f32[512,2,2560]{2,0,1:T(8,128)} async-done(((f32[512,2,2560]{2,0,1:T(8,128)}), f32[512,2,2560]{2,0,1:T(8,128)}, u32[]{:S(2)}, u32[]{:S(2)}) %all-to-all-start) | async-done | bytes 10485792 | tf_op jit(solution)/shard_map/all_to_all | solution.py:50
  394.9 8.6 all-to-all-start.3
  403.5 14.2 %gather_fusion.5 = f32[1024,2560]{1,0:T(8,128)} fusion(f32[1024,2560]{1,0:T(8,128)} %bitcast.10, s32[1024]{0:T(1024)S(1)} %fusion.13), kind=kCustom, calls=%fused_computation.5 | custom fusion | bytes 20975616 | tf_op jit(solution)/shard_map/gather | solution.py:60
  417.8 213.1 %all-to-all-done.3 = f32[16,64,2560]{2,1,0:T(8,128)} async-done(((f32[16,64,2560]{2,1,0:T(8,128)}), f32[16,64,2560]{2,1,0:T(8,128)}, u32[]{:S(2)}, u32[]{:S(2)}) %all-to-all-start.3) | async-done | bytes 10485792 | tf_op jit(solution)/shard_map/all_to_all | solution.py:59
  630.8 4.8 all-to-all-start.7
  635.6 14.2 %gather_fusion = f32[1024,2560]{1,0:T(8,128)} fusion(f32[1024,2560]{1,0:T(8,128)} %bitcast.1, s32[1024]{0:T(1024)S(1)} %fusion.13), kind=kCustom, calls=%fused_computation | custom fusion | bytes 20975616 | tf_op jit(solution)/shard_map/gather | solution.py:58
  649.8 213.1 %all-to-all-done.7 = f32[16,64,2560]{2,1,0:T(8,128)} async-done(((f32[16,64,2560]{2,1,0:T(8,128)}), f32[16,64,2560]{2,1,0:T(8,128)}, u32[]{:S(2)}, u32[]{:S(2)}) %all-to-all-start.7) | async-done | bytes 10485792 | tf_op jit(solution)/shard_map/all_to_all | solution.py:60
  862.9 5.0 all-to-all-start.1
  867.9 0.1 fusion.8
  868.0 7.8 sort.49
  875.7 6.1 gather_fusion.1
  882.6 4.4 sort.50
  887.0 0.6 reduce_sum.29
  888.3 14.2 %gather_fusion.4 = f32[1024,2560]{1,0:T(8,128)} fusion(f32[1024,2560]{1,0:T(8,128)} %bitcast.7, s32[1024]{0:T(1024)S(1)} %fusion.15), kind=kCustom, calls=%fused_computation.4 | custom fusion | bytes 20975616 | tf_op jit(solution)/shard_map/gather | solution.py:65
  902.5 14.2 %gather_fusion.6 = f32[1024,2560]{1,0:T(8,128)} fusion(f32[1024,2560]{1,0:T(8,128)} %bitcast.12, s32[1024]{0:T(1024)S(1)} %fusion.15), kind=kCustom, calls=%fused_computation.6 | custom fusion | bytes 20975616 | tf_op jit(solution)/shard_map/gather | solution.py:66
  916.8 178.2 %all-to-all-done.1 = f32[16,64,2560]{2,1,0:T(8,128)} async-done(((f32[16,64,2560]{2,1,0:T(8,128)}), f32[16,64,2560]{2,1,0:T(8,128)}, u32[]{:S(2)}, u32[]{:S(2)}) %all-to-all-start.1) | async-done | bytes 10485792 | tf_op jit(solution)/shard_map/all_to_all | solution.py:58
  1095.0 14.2 %gather_fusion.2 = f32[1024,2560]{1,0:T(8,128)} fusion(f32[1024,2560]{1,0:T(8,128)} %bitcast.3, s32[1024]{0:T(1024)S(1)} %fusion.15), kind=kCustom, calls=%fused_computation.2 | custom fusion | bytes 20975616 | tf_op jit(solution)/shard_map/gather | solution.py:64
  1109.2 28.4 %multiply_subtract_fusion = (f32[1024,2560]{1,0:T(8,128)}, f32[1024,2560]{1,0:T(8,128)}, f32[1024,2560]{1,0:T(8,128)}, f32[1024,2560]{1,0:T(8,128)}) fusion(f32[1024,2560]{1,0:T(8,128)} %gather_fusion.2, f32[]{:T(128)} %bitcast.13, f32[]{:T(128)} %bitcast.8, bf16[1024,2560]{1,0:T(8,128)(2,1)} %param.9, f32[]{:T(128)S(6)} %min.3, ...), kind=kLoop, calls=%fused_computation.17 | loop fusion | flops 44564480 | bytes 78643216 | tf_op jit(solution)/shard_map/sub | solution.py:27
  (8 shorter events, 0.0 us)
Async XLA Ops:
  13.9 16.9 %all-to-all-start.5 = ((f32[16,1,1]{2,1,0:T(1,128)}), f32[16,1,1]{2,1,0:T(1,128)S(1)}, u32[]{:S(2)}, u32[]{:S(2)}) async-start(f32[16,1,1]{2,1,0:T(1,128)} %broadcast_in_dim.28), calls=%async_computation.5 | async-start | bytes 16384 | tf_op jit(solution)/shard_map/all_to_all | solution.py:61
  30.7 122.2 %all-to-all-start.2 = ((f32[512,2,2560]{2,0,1:T(8,128)}), f32[512,2,2560]{2,0,1:T(8,128)}, u32[]{:S(2)}, u32[]{:S(2)}) async-start(f32[512,2,2560]{2,0,1:T(8,128)} %bitcast.33), calls=%async_computation.2 | async-start | bytes 20971520 | tf_op jit(solution)/shard_map/all_to_all | solution.py:51
  152.9 121.4 %all-to-all-start.6 = ((f32[512,2,2560]{2,0,1:T(8,128)}), f32[512,2,2560]{2,0,1:T(8,128)}, u32[]{:S(2)}, u32[]{:S(2)}) async-start(f32[512,2,2560]{2,0,1:T(8,128)} %bitcast.34), calls=%async_computation.6 | async-start | bytes 20971520 | tf_op jit(solution)/shard_map/all_to_all | solution.py:52
  274.3 7.8 copy-start
  274.3 120.6 %all-to-all-start = ((f32[512,2,2560]{2,0,1:T(8,128)}), f32[512,2,2560]{2,0,1:T(8,128)}, u32[]{:S(2)}, u32[]{:S(2)}) async-start(f32[512,2,2560]{2,0,1:T(8,128)} %bitcast.32), calls=%async_computation | async-start | bytes 20971520 | tf_op jit(solution)/shard_map/all_to_all | solution.py:50
  394.9 235.9 %all-to-all-start.3 = ((f32[16,64,2560]{2,1,0:T(8,128)}), f32[16,64,2560]{2,1,0:T(8,128)}, u32[]{:S(2)}, u32[]{:S(2)}) async-start(f32[16,64,2560]{2,1,0:T(8,128)} %bitcast.31), calls=%async_computation.3 | async-start | bytes 20971520 | tf_op jit(solution)/shard_map/all_to_all | solution.py:59
  630.8 232.1 %all-to-all-start.7 = ((f32[16,64,2560]{2,1,0:T(8,128)}), f32[16,64,2560]{2,1,0:T(8,128)}, u32[]{:S(2)}, u32[]{:S(2)}) async-start(f32[16,64,2560]{2,1,0:T(8,128)} %bitcast.30), calls=%async_computation.7 | async-start | bytes 20971520 | tf_op jit(solution)/shard_map/all_to_all | solution.py:60
  862.9 232.1 %all-to-all-start.1 = ((f32[16,64,2560]{2,1,0:T(8,128)}), f32[16,64,2560]{2,1,0:T(8,128)}, u32[]{:S(2)}, u32[]{:S(2)}) async-start(f32[16,64,2560]{2,1,0:T(8,128)} %bitcast.29), calls=%async_computation.1 | async-start | bytes 20971520 | tf_op jit(solution)/shard_map/all_to_all | solution.py:58
where the time goes:
time: 1140 us
  waiting for transfers between devices  909 us (80%)
  local copies, waits for them, and re-layouts  120 us (11%)
  other arithmetic  51.9 us (5%)
  starting transfers between devices  49.5 us (4%)
    all_to_all x1, waiting for transfers between devices, per_device(): lax.all_to_all(middle[1][send_order], 'fsdp', split_axis=0, concat_axis=0...  213 us
    all_to_all x1, waiting for transfers between devices, per_device(): lax.all_to_all(middle[2][send_order], 'fsdp', split_axis=0, concat_axis=0...  213 us
    all_to_all x1, waiting for transfers between devices, per_device(): lax.all_to_all(middle[0][send_order], 'fsdp', split_axis=0, concat_axis=0...  178 us
    all_to_all x1, waiting for transfers between devices, per_device(): lax.all_to_all(saved_first, 'tp', split_axis=1, concat_axis=0, tiled=True)  106 us
    all_to_all x1, waiting for transfers between devices, per_device(): lax.all_to_all(saved_second, 'tp', split_axis=1, concat_axis=0, tiled=True)  105 us
    all_to_all x1, waiting for transfers between devices, per_device(): lax.all_to_all(saved_master, 'tp', split_axis=1, concat_axis=0, tiled=True)  94.1 us
    sub x1, other arithmetic, adam_update(): return (master - learn_rate * direction, first_new, second_new, direction)  28.4 us
  transfers between devices with their start and end apart: 7, of which 6 were waited for; matrix products, arithmetic and copies ran while one was open for 11% of the time, Pallas kernels for 0%

commit v1 on v0

v1 whole, which is shorter than its diff:
```python
import math

import jax
import jax.numpy as jnp
from jax import lax
from jax.experimental import pallas as pl
from jax.experimental.pallas import tpu as pltpu
from jax.sharding import PartitionSpec as P

beta_one = 0.9
beta_two = 0.95
epsilon = 1e-08
learn_rate = 0.001
weight_decay = 0.1

LANES = 128
WEIGHTS = (2, 3, 5, 6, 4)


def adam_kernel(scalars, master_ref, first_ref, second_ref, grad_ref, *refs):
    master_out, first_out, second_out, direction_out = refs[-4:]
    scale, first_fix, second_fix = scalars[0], scalars[1], scalars[2]
    clipped = scale * grad_ref[...].astype(jnp.float32)
    first_new = beta_one * first_ref[...] + (1.0 - beta_one) * clipped
    second_new = beta_two * second_ref[...] + (1.0 - beta_two) * clipped * clipped
    master = master_ref[...]
    first_hat = first_new / first_fix
    second_hat = second_new / second_fix
    direction = first_hat / (jnp.sqrt(second_hat) + epsilon) + weight_decay * master
    master_out[...] = master - learn_rate * direction
    first_out[...] = first_new
    second_out[...] = second_new
    direction_out[...] = direction


def adam_chunk(scalars, placed, grad, outs, begin, end):
    rows, columns = grad.shape
    unit = LANES if columns % LANES == 0 else columns
    count, first_unit = (end - begin) // unit, begin // unit

    def moved(shift):
        return pl.BlockSpec((rows, unit), lambda j: (0, j + shift))

    earlier = () if outs is None else tuple(outs)
    size = rows * (end - begin)
    return pl.pallas_call(
        adam_kernel,
        grid=(count,),
        out_shape=[jax.ShapeDtypeStruct((rows, columns), jnp.float32)] * 4,
        in_specs=[pl.BlockSpec(memory_space=pltpu.SMEM)]
        + [moved(0), moved(count), moved(2 * count), moved(first_unit)]
        + [pl.BlockSpec(memory_space=pl.ANY)] * len(earlier),
        out_specs=[moved(first_unit)] * 4,
        input_output_aliases={5 + i: i for i in range(len(earlier))},
        cost_estimate=pl.CostEstimate(
            flops=16 * size, bytes_accessed=30 * size, transcendentals=2 * size
        ),
        name="adam",
    )(scalars, placed, placed, placed, grad, *earlier)


def column_chunks(columns):
    unit = LANES if columns % LANES == 0 else 1
    units = columns // unit
    total, reached, edges = sum(WEIGHTS), 0, [0]
    for weight in WEIGHTS:
        reached += weight
        edge = units * reached // total
        if edge > edges[-1]:
            edges.append(edge)
    return [(a * unit, b * unit) for a, b in zip(edges[:-1], edges[1:])]


def per_device(all_rows_total, saved_master, saved_first, saved_second, grad, row_target, step):
    tp_count = lax.axis_size("tp")
    tp_index = lax.axis_index("tp")
    block_index = lax.axis_index("fsdp")
    block_rows, columns = grad.shape
    piece_rows = saved_master.shape[0]
    all_rows = row_target.shape[0]
    saved = (saved_master, saved_first, saved_second)

    mine = lax.dynamic_slice_in_dim(row_target, block_index * block_rows, block_rows)
    send_order = jnp.argsort(mine, stable=True)
    owner = send_order // piece_rows
    send_local = jnp.mod(tp_index - owner, tp_count) * piece_rows + send_order % piece_rows

    in_block = row_target // block_rows == block_index
    sort_keys = jnp.where(in_block, row_target, all_rows)
    source_block = jnp.argsort(sort_keys, stable=True)[:block_rows] // block_rows
    local = jnp.arange(block_rows, dtype=jnp.int32)
    before = (source_block[None, :] == source_block[:, None]) & (local[None, :] < local[:, None])
    pair_rows = block_rows // lax.axis_size("fsdp")
    place_order = source_block * pair_rows + jnp.sum(before.astype(jnp.int32), axis=1)

    def part_of(which, begin, end):
        options = [
            jnp.concatenate(
                [x[:, t * columns + begin : t * columns + end] for x in saved], axis=1
            )
            for t in range(tp_count)
        ]
        result = options[0]
        for t in range(1, tp_count):
            result = jnp.where(which == t, options[t], result)
        return result

    chunks = column_chunks(columns)
    middles = []
    for begin, end in chunks:
        pieces = [part_of(tp_index, begin, end)]
        for shift in range(1, tp_count):
            pairs = [(t, (t + shift) % tp_count) for t in range(tp_count)]
            outgoing = part_of(jnp.mod(tp_index + shift, tp_count), begin, end)
            pieces.append(lax.ppermute(outgoing, "tp", pairs))
        middles.append(pieces)

    grad_wide = grad.astype(jnp.float32)
    squares = lax.all_gather(jnp.sum(grad_wide * grad_wide), ("fsdp", "tp"))
    total = jnp.sum(squares)
    scale = jnp.minimum(1.0, math.sqrt(all_rows_total) / jnp.sqrt(total))

    count = step[0].astype(jnp.float32)
    scalars = jnp.stack(
        [
            scale,
            1.0 - jnp.power(jnp.float32(beta_one), count),
            1.0 - jnp.power(jnp.float32(beta_two), count),
        ]
    )
    arrived, updated = [], []
    for index, pieces in enumerate(middles):
        gathered = jnp.concatenate(pieces, axis=0)[send_local]
        if index >= 2:
            placed = arrived[index - 2][place_order]
            earlier = updated[-1] if updated else None
            updated.append(adam_chunk(scalars, placed, grad, earlier, *chunks[index - 2]))
            gathered, arrived[-1], updated[-1] = lax.optimization_barrier(
                (gathered, arrived[-1], updated[-1])
            )
        elif index == 1:
            gathered, arrived[0] = lax.optimization_barrier((gathered, arrived[0]))
        arrived.append(
            lax.all_to_all(gathered, "fsdp", split_axis=0, concat_axis=0, tiled=True)
        )
    for index in range(len(updated), len(chunks)):
        placed = arrived[index][place_order]
        earlier = updated[-1] if updated else None
        updated.append(adam_chunk(scalars, placed, grad, earlier, *chunks[index]))
    return tuple(updated[-1])


def solution(mesh):
    in_specs = (
        P(("fsdp", "tp"), None),
        P(("fsdp", "tp"), None),
        P(("fsdp", "tp"), None),
        P("fsdp", "tp"),
        P(),
        P(),
    )
    out_specs = (P("fsdp", "tp"), P("fsdp", "tp"), P("fsdp", "tp"), P("fsdp", "tp"))

    def whole(saved_master, saved_first, saved_second, grad, row_target, step):
        def body(*args):
            return per_device(grad.shape[0] * grad.shape[1], *args)

        return jax.shard_map(
            body, mesh=mesh, in_specs=in_specs, out_specs=out_specs, check_vma=False
        )(saved_master, saved_first, saved_second, grad, row_target, step)

    return whole
```

time: 1140 us -> 853 us (0.75)
  waiting for transfers between devices: 909 us -> 488 us
  blocking collectives: 4.95 us -> 116 us
  Pallas kernels: 0 us -> 38.6 us
  starting transfers between devices: 49.5 us -> 37.4 us
    all_to_all x7 -> x5, waiting for transfers between devices: 909 us -> 237 us  [per_device(): lax.all_to_all(gathered, 'fsdp', split_axis=0, concat_axis=0, tiled=True)]
    ppermute x0 -> x5, waiting for transfers between devices: none -> 251 us  [per_device(): pieces.append(lax.ppermute(outgoing, 'tp', pairs))]
    unnamed x0 -> x1, blocking collectives: none -> 116 us
    pallas_call x0 -> x5, Pallas kernels: none -> 38.6 us  [adam_chunk(): pl.pallas_call(adam_kernel, grid=(count,), out_shape=[jax.ShapeDtypeStruc...]
    sub x2 -> x0, other arithmetic: 28.4 us -> none  [the longest x1 28.4 us: adam_update(): return (master - learn_rate * direction, first_new, second_new, direction)]
    all_to_all x3 -> x0, local copies, waits for them, and re-layouts: 26.8 us -> none  [the longest x1 8.93 us: per_device(): lax.all_to_all(saved_second, 'tp', split_axis=1, concat_axis=0, tiled=True)]
    slice x0 -> x10, local copies, waits for them, and re-layouts: none -> 21 us  [part_of(): x[:, t * columns + begin:t * columns + end]]
    all_to_all x7 -> x5, starting transfers between devices: 49.5 us -> 29.8 us  [per_device(): lax.all_to_all(gathered, 'fsdp', split_axis=0, concat_axis=0, tiled=True)]
  transfers between devices with their start and end apart: 7 -> 10, of which waited for: 6 -> 8; matrix products, arithmetic and copies ran while one was open for 11% -> 17% of each run, Pallas kernels for 0% -> 4%
where the time goes in v1:
time: 853 us; the launch traced here: 851 us
  waiting for transfers between devices  488 us (57%)
  local copies, waits for them, and re-layouts  123 us (14%)
  blocking collectives  116 us (14%)
  other arithmetic  45.1 us (5%)
  Pallas kernels  38.6 us (5%)
  starting transfers between devices  37.4 us (4%)
    ppermute x5, waiting for transfers between devices, per_device(): pieces.append(lax.ppermute(outgoing, 'tp', pairs))  251 us
    all_to_all x5, waiting for transfers between devices, per_device(): lax.all_to_all(gathered, 'fsdp', split_axis=0, concat_axis=0, tiled=True)  237 us
    unnamed x1, blocking collectives  116 us
    gather x5, local copies, waits for them, and re-layouts, per_device(): gathered = jnp.concatenate(pieces, axis=0)[send_local]  50.3 us
    pallas_call x5, Pallas kernels, adam_chunk(): pl.pallas_call(adam_kernel, grid=(count,), out_shape=[jax.ShapeDtypeStruc...  38.6 us
    all_to_all x5, starting transfers between devices, per_device(): lax.all_to_all(gathered, 'fsdp', split_axis=0, concat_axis=0, tiled=True)  29.8 us
    gather x3, local copies, waits for them, and re-layouts, per_device(): placed = arrived[index - 2][place_order]  26.3 us
    gather x2, local copies, waits for them, and re-layouts, per_device(): placed = arrived[index][place_order]  24 us
  transfers between devices with their start and end apart: 10, of which 8 were waited for; matrix products, arithmetic and copies ran while one was open for 17% of the time, Pallas kernels for 4%

profile of v1, /device:TPU:11, one launch (start us, length us, event | category | flops | bytes accessed | tf_op | source)
XLA Modules:
  0.0 850.6 jit_solution(11624915638044482750)
XLA Ops:
  0.6 1.3 fusion.26
  1.9 1.7 fusion.24
  3.6 0.0 copy-start.1
  3.6 1.4 fusion.10
  5.0 1.2 collective-permute-start.4
  6.2 4.4 sort.34
  10.6 29.6 %collective-permute-done.4 = f32[512,768]{1,0:T(8,128)S(1)} collective-permute-done((f32[512,768]{1,0:T(8,128)S(1)}, f32[512,768]{1,0:T(8,128)S(1)}, u32[]{:S(2)}, u32[]{:S(2)}) %collective-permute-start.4) | collective-permute-done | bytes 1572896 | tf_op jit(solution)/shard_map/ppermute | solution.py:115
  40.2 1.1 copy-done
  41.4 2.1 pad_maximum_fusion.10
  43.5 5.2 gather_fusion.4
  48.7 7.4 all-to-all-start
  56.1 1.5 fusion.29
  57.6 2.1 fusion.27
  59.6 0.3 fusion.8
  59.9 1.3 collective-permute-start.3
  61.2 51.2 %collective-permute-done.3 = f32[512,1152]{1,0:T(8,128)S(1)} collective-permute-done((f32[512,1152]{1,0:T(8,128)S(1)}, f32[512,1152]{1,0:T(8,128)S(1)}, u32[]{:S(2)}, u32[]{:S(2)}) %collective-permute-start.3) | collective-permute-done | bytes 2359328 | tf_op jit(solution)/shard_map/ppermute | solution.py:115
  112.4 2.5 pad_maximum_fusion.5
  114.9 9.1 %gather_fusion.3 = f32[1024,1152]{1,0:T(8,128)} fusion(f32[1024,1152]{1,0:T(8,128)} %pad_maximum_fusion.5, s32[1024]{0:T(1024)S(1)} %fusion.20), kind=kCustom, calls=%fused_computation.3 | custom fusion | bytes 9441280 | tf_op jit(solution)/shard_map/gather | solution.py:133
  124.0 2.0 all-to-all-done
  126.0 4.9 all-to-all-start.1
  130.9 1.9 fusion.32
  132.7 2.9 fusion.30
  135.6 3.5 fusion.4
  139.1 1.2 collective-permute-start.2
  140.3 5.8 multiply_reduce_fusion
  146.1 0.8 dynamic-update-slice
  146.9 115.7 %all-reduce = f32[32]{0:T(128)S(1)} all-reduce(f32[32]{0:T(128)S(1)} %dynamic-update-slice), channel_id=1, replica_groups=mesh['fsdp'=16,'tp'=2] {'fsdp','tp'}, use_global_device_ids=true, to_apply=%add | all-reduce | flops 32 | bytes 256
  262.6 0.6 reduce_sum.28
  264.7 7.8 sort.35
  272.4 0.6 pad_maximum_fusion.15.scalars
  273.0 0.5 convert_reduce_fusion
  273.6 0.0 collective-permute-done.2
  273.6 7.0 pad_maximum_fusion.1
  280.6 12.0 %gather_fusion.2 = f32[1024,1920]{1,0:T(8,128)} fusion(f32[1024,1920]{1,0:T(8,128)} %pad_maximum_fusion.1, s32[1024]{0:T(1024)S(1)} %fusion.20), kind=kCustom, calls=%fused_computation.2 | custom fusion | bytes 15732736 | tf_op jit(solution)/shard_map/gather | solution.py:133
  292.6 5.3 gather_fusion.5
  297.9 3.9 adam.5
  301.8 7.9 all-to-all-start.2
  309.7 2.1 fusion.35
  311.8 3.3 fusion.33
  315.1 0.7 fusion.2
  315.8 1.9 collective-permute-start.1
  317.8 101.9 %collective-permute-done.1 = f32[512,2304]{1,0:T(8,128)S(1)} collective-permute-done((f32[512,2304]{1,0:T(8,128)S(1)}, f32[512,2304]{1,0:T(8,128)S(1)}, u32[]{:S(2)}, u32[]{:S(2)}) %collective-permute-start.1) | collective-permute-done | bytes 4718624 | tf_op jit(solution)/shard_map/ppermute | solution.py:115
  419.7 4.3 pad_maximum_fusion
  423.9 13.5 %gather_fusion.1 = f32[1024,2304]{1,0:T(8,128)} fusion(f32[1024,2304]{1,0:T(8,128)} %pad_maximum_fusion, s32[1024]{0:T(1024)S(1)} %fusion.20), kind=kCustom, calls=%fused_computation.1 | custom fusion | bytes 18878464 | tf_op jit(solution)/shard_map/gather | solution.py:133
  437.4 9.1 %gather_fusion.6 = f32[1024,1152]{1,0:T(8,128)} fusion(f32[1024,1152]{1,0:T(8,128)} %bitcast.5, s32[1024]{0:T(1024)S(1)} %fusion.21), kind=kCustom, calls=%fused_computation.6 | custom fusion | bytes 9441280 | tf_op jit(solution)/shard_map/gather | solution.py:135
  446.5 6.6 adam.6
  453.1 27.7 %all-to-all-done.2 = f32[16,64,1920]{2,1,0:T(8,128)} async-done(((f32[16,64,1920]{2,1,0:T(8,128)}), f32[16,64,1920]{2,1,0:T(8,128)}, u32[]{:S(2)}, u32[]{:S(2)}) %all-to-all-start.2) | async-done | bytes 7864352 | tf_op jit(solution)/shard_map/all_to_all | solution.py:144
  480.8 4.8 all-to-all-start.3
  485.6 1.7 fusion.38
  487.3 2.6 fusion.36
  489.9 0.6 fusion.6
  490.5 1.9 collective-permute-start
  492.5 68.1 %collective-permute-done = f32[512,1536]{1,0:T(8,128)S(1)} collective-permute-done((f32[512,1536]{1,0:T(8,128)S(1)}, f32[512,1536]{1,0:T(8,128)S(1)}, u32[]{:S(2)}, u32[]{:S(2)}) %collective-permute-start) | collective-permute-done | bytes 3145760 | tf_op jit(solution)/shard_map/ppermute | solution.py:115
  560.6 3.1 pad_maximum_fusion.2
  563.6 10.5 %gather_fusion = f32[1024,1536]{1,0:T(8,128)} fusion(f32[1024,1536]{1,0:T(8,128)} %pad_maximum_fusion.2, s32[1024]{0:T(1024)S(1)} %fusion.20), kind=kCustom, calls=%fused_computation | custom fusion | bytes 12587008 | tf_op jit(solution)/shard_map/gather | solution.py:133
  574.1 12.0 %gather_fusion.7 = f32[1024,1920]{1,0:T(8,128)} fusion(f32[1024,1920]{1,0:T(8,128)} %bitcast.7, s32[1024]{0:T(1024)S(1)} %fusion.21), kind=kCustom, calls=%fused_computation.7 | custom fusion | bytes 15732736 | tf_op jit(solution)/shard_map/gather | solution.py:135
  586.1 10.0 %adam.7 = (f32[1024,2560]{1,0:T(8,128)}, f32[1024,2560]{1,0:T(8,128)}, f32[1024,2560]{1,0:T(8,128)}, f32[1024,2560]{1,0:T(8,128)}) custom-call(f32[3]{0:T(128)} %pad_maximum_fusion.15.scalars, f32[1024,1920]{1,0:T(8,128)} %gather_fusion.7, f32[1024,1920]{1,0:T(8,128)} %gather_fusion.7, ...), custom_call_target="tpu_custom_call", output_to_operand_aliasing={{0}: (5, {}), {1}: (6, {}), {2}: (7, {}), {3}: (8, {})} | custom-call | flops 10485760 | bytes 19660800 | tf_op jit(solution)/shard_map/adam/pallas_call | solution.py:46
  596.1 94.3 %all-to-all-done.3 = f32[16,64,2304]{2,1,0:T(8,128)} async-done(((f32[16,64,2304]{2,1,0:T(8,128)}), f32[16,64,2304]{2,1,0:T(8,128)}, u32[]{:S(2)}, u32[]{:S(2)}) %all-to-all-start.3) | async-done | bytes 9437216 | tf_op jit(solution)/shard_map/all_to_all | solution.py:144
  690.4 4.8 all-to-all-start.4
  695.2 13.5 %gather_fusion.9 = f32[1024,2304]{1,0:T(8,128)} fusion(f32[1024,2304]{1,0:T(8,128)} %bitcast.9, s32[1024]{0:T(1024)S(1)} %fusion.21), kind=kCustom, calls=%fused_computation.9 | custom fusion | bytes 18878464 | tf_op jit(solution)/shard_map/gather | solution.py:147
  708.7 10.8 %adam.8 = (f32[1024,2560]{1,0:T(8,128)}, f32[1024,2560]{1,0:T(8,128)}, f32[1024,2560]{1,0:T(8,128)}, f32[1024,2560]{1,0:T(8,128)}) custom-call(f32[3]{0:T(128)} %pad_maximum_fusion.15.scalars, f32[1024,2304]{1,0:T(8,128)} %gather_fusion.9, f32[1024,2304]{1,0:T(8,128)} %gather_fusion.9, ...), custom_call_target="tpu_custom_call", output_to_operand_aliasing={{0}: (5, {}), {1}: (6, {}), {2}: (7, {}), {3}: (8, {})} | custom-call | flops 12582912 | bytes 23592960 | tf_op jit(solution)/shard_map/adam/pallas_call | solution.py:46
  719.4 113.2 %all-to-all-done.4 = f32[16,64,1536]{2,1,0:T(8,128)} async-done(((f32[16,64,1536]{2,1,0:T(8,128)}), f32[16,64,1536]{2,1,0:T(8,128)}, u32[]{:S(2)}, u32[]{:S(2)}) %all-to-all-start.4) | async-done | bytes 6291488 | tf_op jit(solution)/shard_map/all_to_all | solution.py:144
  832.6 10.5 %gather_fusion.8 = f32[1024,1536]{1,0:T(8,128)} fusion(f32[1024,1536]{1,0:T(8,128)} %bitcast.11, s32[1024]{0:T(1024)S(1)} %fusion.21), kind=kCustom, calls=%fused_computation.8 | custom fusion | bytes 12587008 | tf_op jit(solution)/shard_map/gather | solution.py:147
  843.1 7.3 adam.9
  (11 shorter events, 0.1 us)
Async XLA Ops:
  3.6 2.6 copy-start.1
  5.0 35.3 %collective-permute-start.4 = (f32[512,768]{1,0:T(8,128)S(1)}, f32[512,768]{1,0:T(8,128)S(1)}, u32[]{:S(2)}, u32[]{:S(2)}) collective-permute-start(f32[512,768]{1,0:T(8,128)S(1)} %get-tuple-element.119), channel_id=1, source_target_pairs={{0,1},{1,0},{2,3},{3,2},{4,5},{5,4},{6,7},{7,6},{8,9},{9,8},{10,11... | collective-permute-start | bytes 4718600 | tf_op jit(solution)/shard_map/ppermute | solution.py:115
  40.2 1.1 copy-start
  48.7 77.3 %all-to-all-start = ((f32[16,64,768]{2,1,0:T(8,128)}), f32[16,64,768]{2,1,0:T(8,128)S(1)}, u32[]{:S(2)}, u32[]{:S(2)}) async-start(f32[16,64,768]{2,1,0:T(8,128)} %bitcast.17), calls=%async_computation | async-start | bytes 6291456 | tf_op jit(solution)/shard_map/all_to_all | solution.py:144
  59.9 52.5 %collective-permute-start.3 = (f32[512,1152]{1,0:T(8,128)S(1)}, f32[512,1152]{1,0:T(8,128)S(1)}, u32[]{:S(2)}, u32[]{:S(2)}) collective-permute-start(f32[512,1152]{1,0:T(8,128)S(1)} %get-tuple-element.117), channel_id=1, source_target_pairs={{0,1},{1,0},{2,3},{3,2},{4,5},{5,4},{6,7},{7,6},{8,9},{9,8},{10,11... | collective-permute-start | bytes 7077896 | tf_op jit(solution)/shard_map/ppermute | solution.py:115
  126.0 175.8 %all-to-all-start.1 = ((f32[16,64,1152]{2,1,0:T(8,128)}), f32[16,64,1152]{2,1,0:T(8,128)}, u32[]{:S(2)}, u32[]{:S(2)}) async-start(f32[16,64,1152]{2,1,0:T(8,128)} %bitcast.16), calls=%async_computation.1 | async-start | bytes 9437184 | tf_op jit(solution)/shard_map/all_to_all | solution.py:144
  139.1 134.5 %collective-permute-start.2 = (f32[512,1920]{1,0:T(8,128)}, f32[512,1920]{1,0:T(8,128)}, u32[]{:S(2)}, u32[]{:S(2)}) collective-permute-start(f32[512,1920]{1,0:T(8,128)} %get-tuple-element.113), channel_id=1, source_target_pairs={{0,1},{1,0},{2,3},{3,2},{4,5},{5,4},{6,7},{7,6},{8,9},{9,8},{10,11... | collective-permute-start | bytes 11796488 | tf_op jit(solution)/shard_map/ppermute | solution.py:115
  301.8 179.1 %all-to-all-start.2 = ((f32[16,64,1920]{2,1,0:T(8,128)}), f32[16,64,1920]{2,1,0:T(8,128)}, u32[]{:S(2)}, u32[]{:S(2)}) async-start(f32[16,64,1920]{2,1,0:T(8,128)} %bitcast.14), calls=%async_computation.2 | async-start | bytes 15728640 | tf_op jit(solution)/shard_map/all_to_all | solution.py:144
  315.8 103.9 %collective-permute-start.1 = (f32[512,2304]{1,0:T(8,128)S(1)}, f32[512,2304]{1,0:T(8,128)S(1)}, u32[]{:S(2)}, u32[]{:S(2)}) collective-permute-start(f32[512,2304]{1,0:T(8,128)S(1)} %get-tuple-element.111), channel_id=1, source_target_pairs={{0,1},{1,0},{2,3},{3,2},{4,5},{5,4},{6,7},{7,6},{8,9},{9,8},{10,11... | collective-permute-start | bytes 14155784 | tf_op jit(solution)/shard_map/ppermute | solution.py:115
  480.8 209.6 %all-to-all-start.3 = ((f32[16,64,2304]{2,1,0:T(8,128)}), f32[16,64,2304]{2,1,0:T(8,128)}, u32[]{:S(2)}, u32[]{:S(2)}) async-start(f32[16,64,2304]{2,1,0:T(8,128)} %bitcast.13), calls=%async_computation.3 | async-start | bytes 18874368 | tf_op jit(solution)/shard_map/all_to_all | solution.py:144
  490.5 70.0 %collective-permute-start = (f32[512,1536]{1,0:T(8,128)S(1)}, f32[512,1536]{1,0:T(8,128)S(1)}, u32[]{:S(2)}, u32[]{:S(2)}) collective-permute-start(f32[512,1536]{1,0:T(8,128)S(1)} %get-tuple-element.115), channel_id=1, source_target_pairs={{0,1},{1,0},{2,3},{3,2},{4,5},{5,4},{6,7},{7,6},{8,9},{9,8},{10,11... | collective-permute-start | bytes 9437192 | tf_op jit(solution)/shard_map/ppermute | solution.py:115
  690.4 142.2 %all-to-all-start.4 = ((f32[16,64,1536]{2,1,0:T(8,128)}), f32[16,64,1536]{2,1,0:T(8,128)}, u32[]{:S(2)}, u32[]{:S(2)}) async-start(f32[16,64,1536]{2,1,0:T(8,128)} %bitcast.15), calls=%async_computation.4 | async-start | bytes 12582912 | tf_op jit(solution)/shard_map/all_to_all | solution.py:144

commit v2 on v1

--- a/solution.py
+++ b/solution.py
@@ -14,7 +14,7 @@
 weight_decay = 0.1
 
 LANES = 128
-WEIGHTS = (2, 3, 5, 6, 4)
+WEIGHTS = (2, 3, 4, 5, 4, 2)
 
 
 def adam_kernel(scalars, master_ref, first_ref, second_ref, grad_ref, *refs):
@@ -106,13 +106,19 @@
         return result
 
     chunks = column_chunks(columns)
+    shifts = range(1, tp_count)
+    leaving = [
+        [part_of(jnp.mod(tp_index + shift, tp_count), begin, end) for shift in shifts]
+        for begin, end in chunks
+    ]
     middles = []
-    for begin, end in chunks:
+    for index, (begin, end) in enumerate(chunks):
         pieces = [part_of(tp_index, begin, end)]
-        for shift in range(1, tp_count):
+        for shift, outgoing in zip(shifts, leaving[index]):
             pairs = [(t, (t + shift) % tp_count) for t in range(tp_count)]
-            outgoing = part_of(jnp.mod(tp_index + shift, tp_count), begin, end)
             pieces.append(lax.ppermute(outgoing, "tp", pairs))
+        if index + 1 < len(chunks):
+            pieces, leaving[index + 1] = lax.optimization_barrier((pieces, leaving[index + 1]))
         middles.append(pieces)
 
     grad_wide = grad.astype(jnp.float32)
@@ -131,6 +137,8 @@
     arrived, updated = [], []
     for index, pieces in enumerate(middles):
         gathered = jnp.concatenate(pieces, axis=0)[send_local]
+        if index == 0:
+            gathered, scalars = lax.optimization_barrier((gathered, scalars))
         if index >= 2:
             placed = arrived[index - 2][place_order]
             earlier = updated[-1] if updated else None

time: 853 us -> 830 us (0.973)
  blocking collectives: 116 us -> 63.2 us
  waiting for transfers between devices: 488 us -> 500 us
  local copies, waits for them, and re-layouts: 123 us -> 132 us
    unnamed x1, blocking collectives: 116 us -> 63.2 us
    ppermute x5 -> x6, waiting for transfers between devices: 251 us -> 271 us  [per_device(): pieces.append(lax.ppermute(outgoing, 'tp', pairs))]
    select_n x5 -> x6, other arithmetic: 6.4 us -> 18.7 us  [part_of(): result = jnp.where(which == t, options[t], result)]
    gather x3 -> x4, local copies, waits for them, and re-layouts: 26.3 us -> 36.8 us  [per_device(): placed = arrived[index - 2][place_order]]
    all_to_all x5 -> x6, waiting for transfers between devices: 237 us -> 229 us  [per_device(): lax.all_to_all(gathered, 'fsdp', split_axis=0, concat_axis=0, tiled=True)]
    slice x10 -> x8, local copies, waits for them, and re-layouts: 21 us -> 25.1 us  [part_of(): x[:, t * columns + begin:t * columns + end]]
    gather x5 -> x6, local copies, waits for them, and re-layouts: 50.3 us -> 52.7 us  [per_device(): gathered = jnp.concatenate(pieces, axis=0)[send_local]]
    all_to_all x5 -> x6, starting transfers between devices: 29.8 us -> 31.4 us  [per_device(): lax.all_to_all(gathered, 'fsdp', split_axis=0, concat_axis=0, tiled=True)]
  transfers between devices with their start and end apart: 10 -> 12, of which waited for: 8 -> 11; matrix products, arithmetic and copies ran while one was open for 17% -> 20% of each run, Pallas kernels for 4% -> 4%
where the time goes in v2:
time: 830 us; the launch traced here: 828 us
  waiting for transfers between devices  500 us (60%)
  local copies, waits for them, and re-layouts  132 us (16%)
  blocking collectives  63.2 us (8%)
  other arithmetic  53.4 us (6%)
  Pallas kernels  39.2 us (5%)
  starting transfers between devices  37.9 us (5%)
    ppermute x6, waiting for transfers between devices, per_device(): pieces.append(lax.ppermute(outgoing, 'tp', pairs))  271 us
    all_to_all x6, waiting for transfers between devices, per_device(): lax.all_to_all(gathered, 'fsdp', split_axis=0, concat_axis=0, tiled=True)  229 us
    unnamed x1, blocking collectives  63.2 us
    gather x6, local copies, waits for them, and re-layouts, per_device(): gathered = jnp.concatenate(pieces, axis=0)[send_local]  52.7 us
    pallas_call x6, Pallas kernels, adam_chunk(): pl.pallas_call(adam_kernel, grid=(count,), out_shape=[jax.ShapeDtypeStruc...  39.2 us
    gather x4, local copies, waits for them, and re-layouts, per_device(): placed = arrived[index - 2][place_order]  36.8 us
    all_to_all x6, starting transfers between devices, per_device(): lax.all_to_all(gathered, 'fsdp', split_axis=0, concat_axis=0, tiled=True)  31.4 us
    slice x8, local copies, waits for them, and re-layouts, part_of(): x[:, t * columns + begin:t * columns + end]  25.1 us
  transfers between devices with their start and end apart: 12, of which 11 were waited for; matrix products, arithmetic and copies ran while one was open for 20% of the time, Pallas kernels for 4%

profile of v2, /device:TPU:11, one launch (start us, length us, event | category | flops | bytes accessed | tf_op | source)
XLA Modules:
  0.0 828.4 jit_solution(8863789874913475360)
XLA Ops:
  0.7 2.8 fusion.28
  3.5 3.8 fusion.26
  7.3 1.3 fusion.11
  8.6 1.2 collective-permute-start
  9.9 3.3 multiply_reduce_fusion
  13.9 63.2 %all-reduce = f32[32]{0:T(128)S(1)} all-reduce(f32[32]{0:T(128)S(1)} %dynamic-update-slice), channel_id=1, replica_groups=mesh['fsdp'=16,'tp'=2] {'fsdp','tp'}, use_global_device_ids=true, to_apply=%add | all-reduce | flops 32 | bytes 256
  79.1 4.4 sort.34
  84.1 1.5 fusion.37
  85.6 2.1 fusion.35
  87.7 2.5 fusion.7
  90.2 1.1 copy-done.4
  91.4 1.6 pad_maximum_fusion.6
  93.0 5.2 gather_fusion
  98.2 7.4 all-to-all-start
  106.6 4.0 fusion.31
  110.6 6.2 fusion.29
  116.8 3.0 fusion.3
  119.8 38.5 %collective-permute-done.1 = f32[512,1152]{1,0:T(8,128)S(1)} collective-permute-done((f32[512,1152]{1,0:T(8,128)}, f32[512,1152]{1,0:T(8,128)S(1)}, u32[]{:S(2)}, u32[]{:S(2)}) %collective-permute-start.1) | collective-permute-done | bytes 2359328 | tf_op jit(solution)/shard_map/ppermute | solution.py:119
  158.2 2.5 pad_maximum_fusion.3
  160.7 9.0 %gather_fusion.5 = f32[1024,1152]{1,0:T(8,128)} fusion(f32[1024,1152]{1,0:T(8,128)} %pad_maximum_fusion.3, s32[1024]{0:T(1024)S(1)} %fusion.22), kind=kCustom, calls=%fused_computation.5 | custom fusion | bytes 9441280 | tf_op jit(solution)/shard_map/gather | solution.py:139
  169.8 5.7 all-to-all-done
  175.5 4.8 all-to-all-start.1
  180.3 1.1 collective-permute-start.2
  181.4 7.8 sort.35
  189.7 1.9 fusion.34
  191.6 2.9 fusion.32
  194.5 3.6 fusion.1
  198.1 51.8 %collective-permute-done.2 = f32[512,1536]{1,0:T(8,128)} collective-permute-done((f32[512,1536]{1,0:T(8,128)}, f32[512,1536]{1,0:T(8,128)}, u32[]{:S(2)}, u32[]{:S(2)}) %collective-permute-start.2) | collective-permute-done | bytes 3145760 | tf_op jit(solution)/shard_map/ppermute | solution.py:119
  249.9 5.0 pad_maximum_fusion.2
  255.0 10.6 %gather_fusion.4 = f32[1024,1536]{1,0:T(8,128)} fusion(f32[1024,1536]{1,0:T(8,128)} %pad_maximum_fusion.2, s32[1024]{0:T(1024)S(1)} %fusion.22), kind=kCustom, calls=%fused_computation.4 | custom fusion | bytes 12587008 | tf_op jit(solution)/shard_map/gather | solution.py:139
  265.5 5.3 gather_fusion.6
  270.9 3.9 adam.6
  274.8 9.2 %all-to-all-done.1 = f32[16,64,1152]{2,1,0:T(8,128)} async-done(((f32[16,64,1152]{2,1,0:T(8,128)}), f32[16,64,1152]{2,1,0:T(8,128)}, u32[]{:S(2)}, u32[]{:S(2)}) %all-to-all-start.1) | async-done | bytes 4718624 | tf_op jit(solution)/shard_map/all_to_all | solution.py:152
  284.0 4.8 all-to-all-start.2
  288.8 1.1 collective-permute-start.3
  289.8 4.4 fusion.5
  294.2 81.0 %collective-permute-done.3 = f32[512,1920]{1,0:T(8,128)S(1)} collective-permute-done((f32[512,1920]{1,0:T(8,128)}, f32[512,1920]{1,0:T(8,128)S(1)}, u32[]{:S(2)}, u32[]{:S(2)}) %collective-permute-start.3) | collective-permute-done | bytes 3932192 | tf_op jit(solution)/shard_map/ppermute | solution.py:119
  375.3 3.6 pad_maximum_fusion
  378.9 12.0 %gather_fusion.3 = f32[1024,1920]{1,0:T(8,128)} fusion(f32[1024,1920]{1,0:T(8,128)} %pad_maximum_fusion, s32[1024]{0:T(1024)S(1)} %fusion.22), kind=kCustom, calls=%fused_computation.3 | custom fusion | bytes 15732736 | tf_op jit(solution)/shard_map/gather | solution.py:139
  390.8 9.0 %gather_fusion.7 = f32[1024,1152]{1,0:T(8,128)} fusion(f32[1024,1152]{1,0:T(8,128)} %bitcast.5, s32[1024]{0:T(1024)S(1)} %fusion.23), kind=kCustom, calls=%fused_computation.7 | custom fusion | bytes 9441280 | tf_op jit(solution)/shard_map/gather | solution.py:143
  399.9 6.6 adam.7
  406.5 19.7 %all-to-all-done.2 = f32[16,64,1536]{2,1,0:T(8,128)} async-done(((f32[16,64,1536]{2,1,0:T(8,128)}), f32[16,64,1536]{2,1,0:T(8,128)}, u32[]{:S(2)}, u32[]{:S(2)}) %all-to-all-start.2) | async-done | bytes 6291488 | tf_op jit(solution)/shard_map/all_to_all | solution.py:152
  426.2 4.8 all-to-all-start.3
  432.0 3.8 fusion.10
  435.8 64.8 %collective-permute-done.4 = f32[512,1536]{1,0:T(8,128)S(1)} collective-permute-done((f32[512,1536]{1,0:T(8,128)}, f32[512,1536]{1,0:T(8,128)S(1)}, u32[]{:S(2)}, u32[]{:S(2)}) %collective-permute-start.4) | collective-permute-done | bytes 3145760 | tf_op jit(solution)/shard_map/ppermute | solution.py:119
  500.6 3.1 pad_maximum_fusion.1
  503.7 10.6 %gather_fusion.2 = f32[1024,1536]{1,0:T(8,128)} fusion(f32[1024,1536]{1,0:T(8,128)} %pad_maximum_fusion.1, s32[1024]{0:T(1024)S(1)} %fusion.22), kind=kCustom, calls=%fused_computation.2 | custom fusion | bytes 12587008 | tf_op jit(solution)/shard_map/gather | solution.py:139
  514.2 10.5 %gather_fusion.8 = f32[1024,1536]{1,0:T(8,128)} fusion(f32[1024,1536]{1,0:T(8,128)} %bitcast.7, s32[1024]{0:T(1024)S(1)} %fusion.23), kind=kCustom, calls=%fused_computation.8 | custom fusion | bytes 12587008 | tf_op jit(solution)/shard_map/gather | solution.py:143
  524.8 7.3 adam.8
  532.1 70.0 %all-to-all-done.3 = f32[16,64,1920]{2,1,0:T(8,128)} async-done(((f32[16,64,1920]{2,1,0:T(8,128)}), f32[16,64,1920]{2,1,0:T(8,128)}, u32[]{:S(2)}, u32[]{:S(2)}) %all-to-all-start.3) | async-done | bytes 7864352 | tf_op jit(solution)/shard_map/all_to_all | solution.py:152
  602.1 4.9 all-to-all-start.4
  607.0 1.1 collective-permute-start.5
  608.0 34.7 %collective-permute-done.5 = f32[512,768]{1,0:T(8,128)S(1)} collective-permute-done((f32[512,768]{1,0:T(8,128)S(1)}, f32[512,768]{1,0:T(8,128)S(1)}, u32[]{:S(2)}, u32[]{:S(2)}) %collective-permute-start.5) | collective-permute-done | bytes 1572896 | tf_op jit(solution)/shard_map/ppermute | solution.py:119
  642.7 1.6 pad_maximum_fusion.11
  644.3 5.3 gather_fusion.1
  649.6 11.9 %gather_fusion.9 = f32[1024,1920]{1,0:T(8,128)} fusion(f32[1024,1920]{1,0:T(8,128)} %bitcast.9, s32[1024]{0:T(1024)S(1)} %fusion.23), kind=kCustom, calls=%fused_computation.9 | custom fusion | bytes 15732736 | tf_op jit(solution)/shard_map/gather | solution.py:143
  661.5 10.1 %adam.9 = (f32[1024,2560]{1,0:T(8,128)}, f32[1024,2560]{1,0:T(8,128)}, f32[1024,2560]{1,0:T(8,128)}, f32[1024,2560]{1,0:T(8,128)}) custom-call(f32[3]{0:T(128)} %pad_maximum_fusion.18.scalars, f32[1024,1920]{1,0:T(8,128)} %gather_fusion.9, f32[1024,1920]{1,0:T(8,128)} %gather_fusion.9, ...), custom_call_target="tpu_custom_call", output_to_operand_aliasing={{0}: (5, {}), {1}: (6, {}), {2}: (7, {}), {3}: (8, {})} | custom-call | flops 10485760 | bytes 19660800 | tf_op jit(solution)/shard_map/adam/pallas_call | solution.py:46
  671.6 72.7 %all-to-all-done.4 = f32[16,64,1536]{2,1,0:T(8,128)} async-done(((f32[16,64,1536]{2,1,0:T(8,128)}), f32[16,64,1536]{2,1,0:T(8,128)}, u32[]{:S(2)}, u32[]{:S(2)}) %all-to-all-start.4) | async-done | bytes 6291488 | tf_op jit(solution)/shard_map/all_to_all | solution.py:152
  744.4 4.8 all-to-all-start.5
  749.1 10.5 %gather_fusion.11 = f32[1024,1536]{1,0:T(8,128)} fusion(f32[1024,1536]{1,0:T(8,128)} %bitcast.11, s32[1024]{0:T(1024)S(1)} %fusion.23), kind=kCustom, calls=%fused_computation.11 | custom fusion | bytes 12587008 | tf_op jit(solution)/shard_map/gather | solution.py:155
  759.6 7.3 adam.10
  767.0 52.1 %all-to-all-done.5 = f32[16,64,768]{2,1,0:T(8,128)S(1)} async-done(((f32[16,64,768]{2,1,0:T(8,128)}), f32[16,64,768]{2,1,0:T(8,128)S(1)}, u32[]{:S(2)}, u32[]{:S(2)}) %all-to-all-start.5) | async-done | bytes 3145760 | tf_op jit(solution)/shard_map/all_to_all | solution.py:152
  819.0 5.3 gather_fusion.10
  824.3 3.9 adam.11
  (33 shorter events, 4.7 us)
Async XLA Ops:
  0.6 9.2 %slice-start = ((s8[5242880]{0:T(1024)(128)(4,1)}), s8[4194304]{0:T(1024)(128)(4,1)S(1)}, s32[]{:S(2)}) async-start(s8[5242880]{0:T(1024)(128)(4,1)} %bitcast.14), calls=%async_computation.6 | async-start | bytes 8388608
  3.5 6.4 slice-start.1
  8.6 70.5 %copy-start.6 = (s32[16384]{0:T(1024)S(1)}, s32[16384]{0:T(1024)}, u32[]{:S(2)}) copy-start(s32[16384]{0:T(1024)} %param.10) | copy-start | bytes 196612
  8.6 81.6 %collective-permute-start = (f32[512,768]{1,0:T(8,128)S(1)}, f32[512,768]{1,0:T(8,128)S(1)}, u32[]{:S(2)}, u32[]{:S(2)}) collective-permute-start(f32[512,768]{1,0:T(8,128)S(1)} %get-tuple-element.180), channel_id=1, source_target_pairs={{0,1},{1,0},{2,3},{3,2},{4,5},{5,4},{6,7},{7,6},{8,9},{9,8},{10,11... | collective-permute-start | bytes 4718600 | tf_op jit(solution)/shard_map/ppermute | solution.py:119
  87.7 3.7 copy-start.3
  90.2 1.1 copy-start.4
  98.2 77.3 %all-to-all-start = ((f32[16,64,768]{2,1,0:T(8,128)}), f32[16,64,768]{2,1,0:T(8,128)S(1)}, u32[]{:S(2)}, u32[]{:S(2)}) async-start(f32[16,64,768]{2,1,0:T(8,128)} %bitcast.22), calls=%async_computation | async-start | bytes 6291456 | tf_op jit(solution)/shard_map/all_to_all | solution.py:152
  105.6 52.6 %collective-permute-start.1 = (f32[512,1152]{1,0:T(8,128)}, f32[512,1152]{1,0:T(8,128)S(1)}, u32[]{:S(2)}, u32[]{:S(2)}) collective-permute-start(f32[512,1152]{1,0:T(8,128)} %get-tuple-element.73), channel_id=1, source_target_pairs={{0,1},{1,0},{2,3},{3,2},{4,5},{5,4},{6,7},{7,6},{8,9},{9,8},{10,11... | collective-permute-start | bytes 7077896 | tf_op jit(solution)/shard_map/ppermute | solution.py:119
  116.8 41.4 %copy-start.2 = (f32[512,1152]{1,0:T(8,128)S(1)}, f32[512,1152]{1,0:T(8,128)}, u32[]{:S(2)}) copy-start(f32[512,1152]{1,0:T(8,128)} %get-tuple-element.84) | copy-start | bytes 7077892
  175.5 108.5 %all-to-all-start.1 = ((f32[16,64,1152]{2,1,0:T(8,128)}), f32[16,64,1152]{2,1,0:T(8,128)}, u32[]{:S(2)}, u32[]{:S(2)}) async-start(f32[16,64,1152]{2,1,0:T(8,128)} %bitcast.21), calls=%async_computation.1 | async-start | bytes 9437184 | tf_op jit(solution)/shard_map/all_to_all | solution.py:152
  180.3 69.6 %collective-permute-start.2 = (f32[512,1536]{1,0:T(8,128)}, f32[512,1536]{1,0:T(8,128)}, u32[]{:S(2)}, u32[]{:S(2)}) collective-permute-start(f32[512,1536]{1,0:T(8,128)} %get-tuple-element.74), channel_id=1, source_target_pairs={{0,1},{1,0},{2,3},{3,2},{4,5},{5,4},{6,7},{7,6},{8,9},{9,8},{10,11... | collective-permute-start | bytes 9437192 | tf_op jit(solution)/shard_map/ppermute | solution.py:119
  194.5 55.5 %copy-start.1 = (f32[512,1536]{1,0:T(8,128)S(1)}, f32[512,1536]{1,0:T(8,128)}, u32[]{:S(2)}) copy-start(f32[512,1536]{1,0:T(8,128)} %get-tuple-element.82) | copy-start | bytes 9437188
  284.0 142.2 %all-to-all-start.2 = ((f32[16,64,1536]{2,1,0:T(8,128)}), f32[16,64,1536]{2,1,0:T(8,128)}, u32[]{:S(2)}, u32[]{:S(2)}) async-start(f32[16,64,1536]{2,1,0:T(8,128)} %bitcast.19), calls=%async_computation.2 | async-start | bytes 12582912 | tf_op jit(solution)/shard_map/all_to_all | solution.py:152
  288.8 86.5 %collective-permute-start.3 = (f32[512,1920]{1,0:T(8,128)}, f32[512,1920]{1,0:T(8,128)S(1)}, u32[]{:S(2)}, u32[]{:S(2)}) collective-permute-start(f32[512,1920]{1,0:T(8,128)} %get-tuple-element.75), channel_id=1, source_target_pairs={{0,1},{1,0},{2,3},{3,2},{4,5},{5,4},{6,7},{7,6},{8,9},{9,8},{10,11... | collective-permute-start | bytes 11796488 | tf_op jit(solution)/shard_map/ppermute | solution.py:119
  289.8 85.4 %copy-start = (f32[512,1920]{1,0:T(8,128)S(1)}, f32[512,1920]{1,0:T(8,128)}, u32[]{:S(2)}) copy-start(f32[512,1920]{1,0:T(8,128)} %get-tuple-element.80) | copy-start | bytes 11796484
  426.2 175.9 %all-to-all-start.3 = ((f32[16,64,1920]{2,1,0:T(8,128)}), f32[16,64,1920]{2,1,0:T(8,128)}, u32[]{:S(2)}, u32[]{:S(2)}) async-start(f32[16,64,1920]{2,1,0:T(8,128)} %bitcast.18), calls=%async_computation.3 | async-start | bytes 15728640 | tf_op jit(solution)/shard_map/all_to_all | solution.py:152
  430.9 69.6 %collective-permute-start.4 = (f32[512,1536]{1,0:T(8,128)}, f32[512,1536]{1,0:T(8,128)S(1)}, u32[]{:S(2)}, u32[]{:S(2)}) collective-permute-start(f32[512,1536]{1,0:T(8,128)} %get-tuple-element.76), channel_id=1, source_target_pairs={{0,1},{1,0},{2,3},{3,2},{4,5},{5,4},{6,7},{7,6},{8,9},{9,8},{10,11... | collective-permute-start | bytes 9437192 | tf_op jit(solution)/shard_map/ppermute | solution.py:119
  602.0 4.9 copy-start.5
  602.1 142.3 %all-to-all-start.4 = ((f32[16,64,1536]{2,1,0:T(8,128)}), f32[16,64,1536]{2,1,0:T(8,128)}, u32[]{:S(2)}, u32[]{:S(2)}) async-start(f32[16,64,1536]{2,1,0:T(8,128)} %bitcast.20), calls=%async_computation.4 | async-start | bytes 12582912 | tf_op jit(solution)/shard_map/all_to_all | solution.py:152
  607.0 35.7 %collective-permute-start.5 = (f32[512,768]{1,0:T(8,128)S(1)}, f32[512,768]{1,0:T(8,128)S(1)}, u32[]{:S(2)}, u32[]{:S(2)}) collective-permute-start(f32[512,768]{1,0:T(8,128)S(1)} %copy-done.5), channel_id=1, source_target_pairs={{0,1},{1,0},{2,3},{3,2},{4,5},{5,4},{6,7},{7,6},{8,9},{9,8},{10,11... | collective-permute-start | bytes 4718600 | tf_op jit(solution)/shard_map/ppermute | solution.py:119
  744.4 74.7 %all-to-all-start.5 = ((f32[16,64,768]{2,1,0:T(8,128)}), f32[16,64,768]{2,1,0:T(8,128)S(1)}, u32[]{:S(2)}, u32[]{:S(2)}) async-start(f32[16,64,768]{2,1,0:T(8,128)} %bitcast.23), calls=%async_computation.5 | async-start | bytes 6291456 | tf_op jit(solution)/shard_map/all_to_all | solution.py:152
